TPU v7x, 32 devices: a whole 2x2x4 slice. The times are simulated.
32 devices in a mesh: group: 2 (over x), surf: 16 (over z, y, core).
Axes of the slice: x: 2, y: 2, z: 4, core: 2. Of those that a mesh axis runs over, the one named last changes fastest.
Arguments:
- traces: bfloat16 [4096, 128, 1024], P('surf', 'group'), parts along dimension 1, may hold values from -6 to 6
- operator: bfloat16 [4096, 8, 2, 4096], P('surf'), may hold values from -1 to 1, as said below
- freq_bins: int32 [8], replicated, may hold values from 1 to 511, as said below
- win_lengths: int32 [16], replicated, may hold values from 1 to 96, 1024 in all
- coefficients: float32 [16, 31], replicated, may hold values from -2.5 to 2.5
- neighbour: int32 [4096], P('surf'), may hold values from -2 to 2, as said below
Outputs:
- demultiple: bfloat16 [4096, 128, 1024], P('surf', 'group'), parts along dimension 1
There are 2 independent parts, one for each index of `group`. A program takes and returns all parts, laid end to end along the dimension named above; an argument that names none is the same for every part. Nothing has to cross between parts.
Inputs may be any that keep to these rules, and one draw needn't show every extreme that they name: operator[i, f, c, j] equals operator[j, f, c, i] (reciprocity). `freq_bins`: the 8 bins are distinct. `neighbour`: points of even index take an offset of -2 or -1, points of odd index 1 or 2.
All inputs are finite; a program needn't handle non-finite values.
Results may differ from a plain program's by a relative error of at most 0.004.
Values may be sent and summed in bfloat16 or wider, within the bound.
No kernel may reach another device: no remote copies, remote signals or barrier semaphores. Data moves between devices by JAX's collectives and lax.ppermute only.
A program may use at most 192 MiB of HBM per device.

v0:
```python
import math

import jax
import jax.numpy as jnp
from jax import lax
from jax.sharding import PartitionSpec as P

TAPS = 31
HALO = 2


def padded_2(x, sides, width):
    for axis, dim in sides:
        size, length = (lax.axis_size(axis), x.shape[dim])
        up = [(i, (i + 1) % size) for i in range(size - 1)]
        down = [(j, i) for i, j in up]
        last = lax.slice_in_dim(x, length - width, length, axis=dim)
        initial = lax.slice_in_dim(x, 0, width, axis=dim)
        before = lax.ppermute(last, axis, up)
        after = lax.ppermute(initial, axis, down)
        x = jnp.concatenate([before, x, after], axis=dim)
    return x


def angle_grid(freq_bins, samples):
    sample_index = jnp.arange(samples, dtype=jnp.int32)
    phases = sample_index[:, None] * freq_bins[None, :] % samples
    return 2.0 * math.pi / samples * phases.astype(jnp.float32)


def combine_complex_parts(products):
    real_part = products[:, :, 0, 0] - products[:, :, 1, 1]
    imag_part = products[:, :, 0, 1] + products[:, :, 1, 0]
    return jnp.stack([real_part, imag_part], axis=2)


def matching(multiple_estimate, coefficients, win_lengths):
    samples = multiple_estimate.shape[2]
    half_taps = (TAPS - 1) // 2
    window_ends = jnp.cumsum(win_lengths)
    sample_index = jnp.arange(samples, dtype=jnp.int32)
    window = jnp.sum((window_ends[None, :] <= sample_index[:, None]).astype(jnp.int32), axis=1)
    membership = (
        window[:, None] == jnp.arange(coefficients.shape[0], dtype=jnp.int32)[None, :]
    ).astype(jnp.float32)
    per_sample = jnp.dot(membership, coefficients, precision=lax.Precision.HIGHEST)
    padded = jnp.pad(multiple_estimate, ((0, 0), (0, 0), (half_taps, half_taps)))
    summed = jnp.zeros_like(multiple_estimate)
    for lag_index in range(TAPS):
        summed = summed + per_sample[:, lag_index] * padded[:, :, lag_index : lag_index + samples]
    return summed


def to_traces(spectral_domain, basis):
    point_count, freq_count, parts_count, shot_count = spectral_domain.shape
    rows = spectral_domain.transpose(0, 3, 1, 2).reshape(
        point_count * shot_count, freq_count * parts_count
    )
    timed = jnp.dot(rows, basis, precision=lax.Precision.HIGHEST)
    return timed.reshape(point_count, shot_count, basis.shape[1])


def neighbour_mix(central, padded, neighbour):
    row_count = central.shape[0]
    summed = central
    for offset in range(-HALO, HALO + 1):
        selector = (
            (neighbour == offset)
            .astype(jnp.float32)
            .reshape((row_count,) + (1,) * (central.ndim - 1))
        )
        summed = summed + 0.5 * selector * padded[HALO + offset : HALO + offset + row_count]
    return summed


def on_device(traces, operator, freq_bins, win_lengths, coefficients, neighbour):
    local_points, shot_count, samples = traces.shape
    freq_count = freq_bins.shape[0]
    angles = angle_grid(freq_bins, samples)
    forward = (
        jnp.stack([jnp.cos(angles), -jnp.sin(angles)], axis=2)
        .reshape(samples, 2 * freq_count)
        .astype(jnp.bfloat16)
    )
    spectra = jnp.dot(
        traces.reshape(local_points * shot_count, samples),
        forward,
        preferred_element_type=jnp.float32,
    ).astype(jnp.bfloat16)
    spectra = spectra.reshape(local_points, shot_count, freq_count, 2).transpose(0, 2, 3, 1)
    products = jnp.einsum("cfar,cfbs->rfabs", operator, spectra, preferred_element_type=jnp.float32)
    predicted_multiples = lax.psum_scatter(
        combine_complex_parts(products).reshape(
            lax.axis_size("surf") * local_points, freq_count * 2 * shot_count
        ),
        "surf",
        scatter_dimension=0,
        tiled=True,
    )
    predicted_multiples = predicted_multiples.reshape(local_points, freq_count, 2, shot_count)
    norm_divisor = (2.0 * freq_count * samples) ** (-0.5)
    inverse_transform = norm_divisor * jnp.stack([jnp.cos(angles.T), -jnp.sin(angles.T)], axis=1)
    basis = matching(
        inverse_transform.reshape(2 * freq_count, 1, samples), coefficients, win_lengths
    ).reshape(2 * freq_count, samples)
    padded = padded_2(predicted_multiples.astype(jnp.bfloat16), (("surf", 0),), HALO).astype(
        predicted_multiples.dtype
    )
    mixed = neighbour_mix(predicted_multiples, padded, neighbour)
    adapted = to_traces(mixed, basis)
    return (traces.astype(jnp.float32) - adapted).astype(jnp.bfloat16)


def solution(mesh):
    return jax.shard_map(
        on_device,
        mesh=mesh,
        in_specs=(P("surf", "group", None), P("surf", None, None, None), P(), P(), P(), P("surf")),
        out_specs=P("surf", "group", None),
        check_vma=False,
    )
```

profile of v0, /device:TPU:1, one launch (start us, length us, event | category | flops | bytes accessed | tf_op | source)
XLA Modules:
  0.0 431.1 jit_solution(694189632699482941)
XLA Ops:
  6.5 0.0 copy-start
  6.5 0.0 reduce-scatter.2.cloned.1.call-start
  6.5 0.9 cosine_convert_fusion
  7.5 14.1 %fusion.2 = bf16[16384,16]{0,1:T(8,128)(2,1)S(1)} fusion(bf16[1024,16]{0,1:T(8,128)(2,1)S(1)} %convert_element_type.69, bf16[16384,1024]{1,0:T(8,128)(2,1)} %bitcast.77), kind=kOutput, calls=%fused_computation.4 | convolution fusion | flops 537133056 | bytes 34111488 | tf_op jit(solution)/shard_map/dot_general | solution.py:85
  21.6 1.1 reshape.430
  22.7 32.5 %fusion.3 = f32[4096,8,2,2,64]{0,4,2,3,1:T(8,128)} fusion(bf16[256,8,2,4096,1]{3,2,1,0,4:T(2,128)(2,1)} %bitcast.79, bf16[256,64,8,2]{1,0,3,2:T(8,128)(2,1)S(1)} %reshape.430), kind=kOutput, calls=%fused_computation.6 | convolution fusion | flops 4294967296 | bytes 67633152 | tf_op jit(solution)/shard_map/cfar,cfbs->rfabs/dot_general | solution.py:91
  55.2 11.1 %fusion.6 = f32[4096,8,1,64]{0,3,1,2:T(8,128)} fusion(f32[4096,8,2,2,64]{0,4,2,3,1:T(8,128)} %fusion.3), kind=kLoop, calls=%fused_computation.8 | loop fusion | flops 2097152 | bytes 25165824 | tf_op jit(solution)/shard_map/add | solution.py:33
  66.3 11.1 %fusion.8 = f32[4096,8,1,64]{0,3,1,2:T(8,128)} fusion(f32[4096,8,2,2,64]{0,4,2,3,1:T(8,128)} %fusion.3), kind=kLoop, calls=%fused_computation.11 | loop fusion | flops 2097152 | bytes 25165824 | tf_op jit(solution)/shard_map/sub | solution.py:32
  77.5 6.6 %pad_maximum_fusion = f32[4096,8,2,64]{0,3,1,2:T(8,128)S(1)} fusion(f32[4096,8,1,64]{0,3,1,2:T(8,128)} %fusion.6, f32[4096,8,1,64]{0,3,1,2:T(8,128)} %fusion.8), kind=kLoop, calls=%fused_computation.5 | loop fusion | flops 4194304 | bytes 33554432 | tf_op jit(solution)/shard_map/stack | solution.py:34
  84.1 6.2 %copy.48 = f32[4096,8,2,64]{0,3,2,1:T(8,128)} copy(f32[4096,8,2,64]{0,3,1,2:T(8,128)S(1)} %pad_maximum_fusion) | data formatting | bytes 33554432 | tf_op jit(solution)/shard_map/stack | solution.py:34
  90.3 0.0 copy-start.3
  90.3 0.0 copy-start.1
  90.3 0.0 copy-start.2
  90.3 0.0 reduce-scatter.2.cloned.1.call-update
  90.3 0.6 copy-done.3
  90.9 0.1 copy.49
  91.1 0.1 reduce
  91.2 0.0 copy-done.1
  91.2 0.2 fusion.130
  91.4 0.1 copy.50
  91.5 0.1 convert_reduce_fusion
  91.6 0.0 copy-done
  91.6 0.5 fusion.16
  92.2 0.1 fusion.133
  92.3 177.1 %reduce-scatter.2.cloned.1.call-done = f32[256,1024]{0,1:T(8,128)} async-done(((f32[4096,1024]{0,1:T(8,128)}), f32[256,1024]{0,1:T(8,128)}) %reduce-scatter.2.cloned.1.call-update) | async-done | bytes 1048592 | tf_op jit(solution)/shard_map/reduce_scatter | solution.py:92
  269.4 1.3 convert_element_type.72
  270.6 0.1 fusion.132
  270.8 4.0 collective-permute-start
  274.8 1.9 collective-permute-start.1
  276.7 0.0 copy-done.2
  276.7 1.3 collective-permute-done
  278.1 4.4 %collective-permute-done.1 = bf16[2,8,2,64]{0,3,2,1:T(8,128)(2,1)S(1)} collective-permute-done((bf16[2,8,2,64]{0,3,2,1:T(8,128)(2,1)S(1)}, bf16[2,8,2,64]{0,3,2,1:T(8,128)(2,1)S(1)}, u32[]{:S(2)}, u32[]{:S(2)}) %collective-permute-start.1) | collective-permute-done | bytes 4128 | tf_op jit(solution)/shard_map/ppermute | solution.py:20
  282.5 0.5 maximum_convert_fusion
  282.9 2.4 fusion.9
  285.3 108.1 %subtract_convert_fusion = bf16[256,64,1024]{2,0,1:T(8,128)(2,1)} fusion(bf16[256,64,1024]{2,1,0:T(8,128)(2,1)} %param.6, f32[256,64,16]{0,1,2:T(8,128)S(1)} %bitcast.80, f32[16,1,1024]{2,0,1:T(8,128)S(1)} %broadcast_multiply_fusion, f32[16,1,1024]{2,0,1:T(8,128)S(1)} %stack.21, f32[1024]{0:T(1024)S(1)} %bitcast.96, f32[1024]{0:T(1024)S(1)} %bitcast.97, ...), kind=kOutput, calls=%fused_computation | convolution fusion | flops 3272556544 | bytes 68415488 | tf_op jit(solution)/shard_map/dot_general | solution.py:59
  393.4 30.8 %copy.52 = bf16[256,64,1024]{2,1,0:T(8,128)(2,1)} copy(bf16[256,64,1024]{2,0,1:T(8,128)(2,1)} %subtract_convert_fusion) | data formatting | bytes 67108864 | tf_op jit(solution)/shard_map/convert_element_type | solution.py:111
  (9 shorter events, 0.2 us)
Async XLA Ops:
  6.5 85.1 %copy-start = (f32[16,31]{1,0:T(8,128)S(1)}, f32[16,31]{1,0:T(8,128)}, u32[]{:S(2)}) copy-start(f32[16,31]{1,0:T(8,128)} %param.10) | copy-start | bytes 5956
  6.5 262.8 %reduce-scatter.2.cloned.1.call-start = ((), (), s32[]{:S(2)}) async-start(), calls=%async_computation.1 | async-start | bytes 17825792 | tf_op jit(solution)/shard_map/reduce_scatter | solution.py:92
  90.3 0.7 copy-start.3
  90.3 0.9 copy-start.1
  90.3 186.4 %copy-start.2 = (s32[256]{0:T(256)S(1)}, s32[256]{0:T(256)}, u32[]{:S(2)}) copy-start(s32[256]{0:T(256)} %param.11) | copy-start | bytes 3076
  270.8 7.3 %collective-permute-start = (bf16[2,8,2,64]{0,3,2,1:T(8,128)(2,1)S(1)}, bf16[2,8,2,64]{0,3,2,1:T(8,128)(2,1)S(1)}, u32[]{:S(2)}, u32[]{:S(2)}) collective-permute-start(bf16[2,8,2,64]{0,3,2,1:T(8,128)(2,1)S(1)} %get-tuple-element.5), channel_id=1, source_target_pairs={{0,1},{1,2},{2,3},{3,4},{4,5},{5,6},{6,7},{7,8},{8,9},{9,10},{10,1... | collective-permute-start | bytes 12296 | tf_op jit(solution)/shard_map/ppermute | solution.py:19
  274.8 7.7 %collective-permute-start.1 = (bf16[2,8,2,64]{0,3,2,1:T(8,128)(2,1)S(1)}, bf16[2,8,2,64]{0,3,2,1:T(8,128)(2,1)S(1)}, u32[]{:S(2)}, u32[]{:S(2)}) collective-permute-start(bf16[2,8,2,64]{0,3,2,1:T(8,128)(2,1)S(1)} %get-tuple-element.6), channel_id=1, source_target_pairs={{1,0},{2,1},{3,2},{4,3},{5,4},{6,5},{7,6},{8,7},{9,8},{10,9},{11,1... | collective-permute-start | bytes 12296 | tf_op jit(solution)/shard_map/ppermute | solution.py:20
Sparse Core Ops, SparseCore 0:
  90.4 178.8 reduce-scatter.1
where the time goes:
time: 431 us
  waiting for transfers between devices  183 us (42%)
  matrix products  155 us (36%)
  local copies, waits for them, and re-layouts  39.2 us (9%)
  other arithmetic  34.4 us (8%)
  between operations  13.6 us (3%)
  starting transfers between devices  5.89 us (1%)
    reduce_scatter x1, waiting for transfers between devices, on_device(): lax.psum_scatter(combine_complex_parts(products).reshape(lax.axis_size('s...  177 us
    dot_general x1, matrix products, to_traces(): timed = jnp.dot(rows, basis, precision=lax.Precision.HIGHEST)  108 us
    dot_general x1, matrix products, on_device(): jnp.einsum('cfar,cfbs->rfabs', operator, spectra, preferred_element_type=...  32.5 us
    convert_element_type x1, local copies, waits for them, and re-layouts, on_device(): return (traces.astype(jnp.float32) - adapted).astype(jnp.bfloat16)  30.8 us
    dot_general x1, matrix products, on_device(): jnp.dot(traces.reshape(local_points * shot_count, samples), forward, pref...  14.1 us
    sub x1, other arithmetic, combine_complex_parts(): real_part = products[:, :, 0, 0] - products[:, :, 1, 1]  11.1 us
    add x1, other arithmetic, combine_complex_parts(): imag_part = products[:, :, 0, 1] + products[:, :, 1, 0]  11.1 us
  transfers between devices with their start and end apart: 3, of which 3 were waited for; matrix products, arithmetic and copies ran while one was open for 0% of the time, Pallas kernels for 0%

commit v1 on v0

--- a/solution.py
+++ b/solution.py
@@ -88,16 +88,9 @@
         preferred_element_type=jnp.float32,
     ).astype(jnp.bfloat16)
     spectra = spectra.reshape(local_points, shot_count, freq_count, 2).transpose(0, 2, 3, 1)
-    products = jnp.einsum("cfar,cfbs->rfabs", operator, spectra, preferred_element_type=jnp.float32)
-    predicted_multiples = lax.psum_scatter(
-        combine_complex_parts(products).reshape(
-            lax.axis_size("surf") * local_points, freq_count * 2 * shot_count
-        ),
-        "surf",
-        scatter_dimension=0,
-        tiled=True,
-    )
-    predicted_multiples = predicted_multiples.reshape(local_points, freq_count, 2, shot_count)
+    gathered = lax.all_gather(spectra, "surf", axis=0, tiled=True)
+    products = jnp.einsum("rfac,cfbs->rfabs", operator, gathered, preferred_element_type=jnp.float32)
+    predicted_multiples = combine_complex_parts(products)
     norm_divisor = (2.0 * freq_count * samples) ** (-0.5)
     inverse_transform = norm_divisor * jnp.stack([jnp.cos(angles.T), -jnp.sin(angles.T)], axis=1)
     basis = matching(

time: 431 us -> 319 us (0.74)
  waiting for transfers between devices: 183 us -> 84.7 us
  other arithmetic: 34.4 us -> 3.32 us
  matrix products: 155 us -> 179 us
  local copies, waits for them, and re-layouts: 39.2 us -> 33.6 us
    reduce_scatter x1 -> x0, waiting for transfers between devices: 177 us -> none  [on_device(): lax.psum_scatter(combine_complex_parts(products).reshape(lax.axis_size('s...]
    all_gather x0 -> x1, waiting for transfers between devices: none -> 79 us  [on_device(): gathered = lax.all_gather(spectra, 'surf', axis=0, tiled=True)]
    dot_general x1, matrix products: 32.5 us -> 56.2 us  [on_device(): jnp.einsum('rfac,cfbs->rfabs', operator, gathered, preferred_element_type...]
    sub x1, other arithmetic: 11.1 us -> 0.08 us  [combine_complex_parts(): real_part = products[:, :, 0, 0] - products[:, :, 1, 1]]
    add x1, other arithmetic: 11.1 us -> 0.08 us  [combine_complex_parts(): imag_part = products[:, :, 0, 1] + products[:, :, 1, 0]]
    another operation x4 -> x3, other arithmetic: 7.62 us -> 1.09 us  [the longest x1 6.59 us: combine_complex_parts(): return jnp.stack([real_part, imag_part], axis=2)]
    another operation x2 -> x1, local copies, waits for them, and re-layouts: 6.31 us -> 0.08 us  [the longest x1 6.22 us: combine_complex_parts(): return jnp.stack([real_part, imag_part], axis=2)]
where the time goes in v1:
time: 319 us
  matrix products  179 us (56%)
  waiting for transfers between devices  84.7 us (27%)
  local copies, waits for them, and re-layouts  33.6 us (11%)
  between operations  13.6 us (4%)
  starting transfers between devices  5.14 us (2%)
  other arithmetic  3.32 us (1%)
    dot_general x1, matrix products, to_traces(): timed = jnp.dot(rows, basis, precision=lax.Precision.HIGHEST)  108 us
    all_gather x1, waiting for transfers between devices, on_device(): gathered = lax.all_gather(spectra, 'surf', axis=0, tiled=True)  79 us
    dot_general x1, matrix products, on_device(): jnp.einsum('rfac,cfbs->rfabs', operator, gathered, preferred_element_type...  56.2 us
    convert_element_type x1, local copies, waits for them, and re-layouts, on_device(): return (traces.astype(jnp.float32) - adapted).astype(jnp.bfloat16)  30.8 us
    dot_general x1, matrix products, on_device(): jnp.dot(traces.reshape(local_points * shot_count, samples), forward, pref...  14.1 us
  transfers between devices with their start and end apart: 3, of which 3 were waited for; matrix products, arithmetic and copies ran while one was open for 0% of the time, Pallas kernels for 0%

profile of v1, /device:TPU:1, one launch (start us, length us, event | category | flops | bytes accessed | tf_op | source)
XLA Modules:
  0.0 319.2 jit_solution(13178327084625688040)
XLA Ops:
  6.5 0.0 copy-start
  6.5 0.0 copy-start.2
  6.5 0.0 copy-start.4
  6.5 0.0 all-gather.2.cloned.1.call-start
  6.5 0.9 cosine_convert_fusion
  7.6 14.1 %fusion.2 = bf16[16384,16]{0,1:T(8,128)(2,1)S(1)} fusion(bf16[1024,16]{0,1:T(8,128)(2,1)S(1)} %convert_element_type.69, bf16[16384,1024]{1,0:T(8,128)(2,1)} %bitcast.76), kind=kOutput, calls=%fused_computation.4 | convolution fusion | flops 537133056 | bytes 34111488 | tf_op jit(solution)/shard_map/dot_general | solution.py:85
  21.6 0.0 copy-start.3
  21.6 1.1 reshape.424
  22.8 1.2 copy.44
  23.9 0.0 all-gather.2.cloned.1.call-update
  24.0 0.0 copy-done.4
  24.0 0.1 copy.49
  24.1 0.1 reduce
  24.2 0.0 copy-done.2
  24.2 0.2 fusion.134
  24.4 0.1 copy.50
  24.6 0.1 convert_reduce_fusion
  24.6 0.0 copy-done
  24.7 0.5 fusion.20
  25.2 0.1 fusion.137
  25.3 79.0 %all-gather.2.cloned.1.call-done = bf16[4096,8,2,64]{0,3,2,1:T(8,128)(2,1)} async-done(((bf16[256,8,2,64]{0,3,2,1:T(8,128)(2,1)}), bf16[4096,8,2,64]{0,3,2,1:T(8,128)(2,1)}) %all-gather.2.cloned.1.call-update) | async-done | bytes 8388624 | tf_op jit(solution)/shard_map/all_gather | solution.py:91
  104.3 56.2 %fusion.4 = f32[256,8,2,2,64]{0,4,2,3,1:T(8,128)S(1)} fusion(bf16[256,8,2,4096,1]{3,2,1,0,4:T(2,128)(2,1)} %bitcast.111, bf16[4096,8,2,64]{0,3,2,1:T(8,128)(2,1)} %all-gather.2.cloned.1.call-done), kind=kOutput, calls=%fused_computation.6 | convolution fusion | flops 4294967296 | bytes 44040192 | tf_op jit(solution)/shard_map/rfac,cfbs->rfabs/dot_general | solution.py:92
  160.5 0.1 fusion.17
  160.5 0.1 fusion.19
  160.6 0.1 fusion.16
  160.7 0.1 fusion.136
  160.9 3.2 %collective-permute-start = (bf16[2,8,2,64]{0,3,1,2:T(8,128)(2,1)S(1)}, bf16[2,8,2,64]{0,3,1,2:T(8,128)(2,1)S(1)}, u32[]{:S(2)}, u32[]{:S(2)}) collective-permute-start(bf16[2,8,2,64]{0,3,1,2:T(8,128)(2,1)S(1)} %get-tuple-element.5), channel_id=1, source_target_pairs={{0,1},{1,2},{2,3},{3,4},{4,5},{5,6},{6,7},{7,8},{8,9},{9,10},{10,1... | collective-permute-start | bytes 12296 | tf_op jit(solution)/shard_map/ppermute | solution.py:19
  164.1 1.9 collective-permute-start.1
  166.0 0.0 copy-done.3
  166.0 1.3 collective-permute-done
  167.4 4.4 %collective-permute-done.1 = bf16[2,8,2,64]{0,3,1,2:T(8,128)(2,1)S(1)} collective-permute-done((bf16[2,8,2,64]{0,3,1,2:T(8,128)(2,1)S(1)}, bf16[2,8,2,64]{0,3,1,2:T(8,128)(2,1)S(1)}, u32[]{:S(2)}, u32[]{:S(2)}) %collective-permute-start.1) | collective-permute-done | bytes 4128 | tf_op jit(solution)/shard_map/ppermute | solution.py:20
  171.8 0.5 maximum_convert_fusion
  172.2 1.2 fusion.10
  173.4 0.1 copy.48
  173.5 0.0 copy-start.1
  173.5 108.1 %subtract_convert_fusion = bf16[256,64,1024]{2,0,1:T(8,128)(2,1)} fusion(bf16[256,64,1024]{2,1,0:T(8,128)(2,1)} %param.6, f32[256,64,16]{0,1,2:T(8,128)S(1)} %bitcast.77, f32[16,1,1024]{2,0,1:T(8,128)S(1)} %broadcast_multiply_fusion, f32[16,1,1024]{2,0,1:T(8,128)S(1)} %stack.21, f32[1024]{0:T(1024)S(1)} %bitcast.92, f32[1024]{0:T(1024)S(1)} %bitcast.93, ...), kind=kOutput, calls=%fused_computation | convolution fusion | flops 3272556544 | bytes 68415488 | tf_op jit(solution)/shard_map/dot_general | solution.py:59
  281.6 30.8 %copy.52 = bf16[256,64,1024]{2,1,0:T(8,128)(2,1)} copy(bf16[256,64,1024]{2,0,1:T(8,128)(2,1)} %subtract_convert_fusion) | data formatting | bytes 67108864 | tf_op jit(solution)/shard_map/convert_element_type | solution.py:104
  312.4 0.0 copy-done.1
  (9 shorter events, 0.2 us)
Async XLA Ops:
  6.5 18.1 %copy-start = (f32[16,31]{1,0:T(8,128)S(1)}, f32[16,31]{1,0:T(8,128)}, u32[]{:S(2)}) copy-start(f32[16,31]{1,0:T(8,128)} %param.10) | copy-start | bytes 5956
  6.5 17.7 %copy-start.2 = (s32[8]{0:T(128)S(1)}, s32[8]{0:T(128)}, u32[]{:S(2)}) copy-start(s32[8]{0:T(128)} %param.8) | copy-start | bytes 100
  6.5 17.4 %copy-start.4 = (s32[16]{0:T(128)S(1)}, s32[16]{0:T(128)}, u32[]{:S(2)}) copy-start(s32[16]{0:T(128)} %param.9) | copy-start | bytes 196
  6.5 97.8 %all-gather.2.cloned.1.call-start = ((), (), s32[]{:S(2)}) async-start(), calls=%async_computation | async-start | bytes 8912896 | tf_op jit(solution)/shard_map/all_gather | solution.py:91
  21.6 144.4 %copy-start.3 = (s32[256]{0:T(256)S(1)}, s32[256]{0:T(256)}, u32[]{:S(2)}) copy-start(s32[256]{0:T(256)} %param.11) | copy-start | bytes 3076
  160.9 6.5 %collective-permute-start = (bf16[2,8,2,64]{0,3,1,2:T(8,128)(2,1)S(1)}, bf16[2,8,2,64]{0,3,1,2:T(8,128)(2,1)S(1)}, u32[]{:S(2)}, u32[]{:S(2)}) collective-permute-start(bf16[2,8,2,64]{0,3,1,2:T(8,128)(2,1)S(1)} %get-tuple-element.5), channel_id=1, source_target_pairs={{0,1},{1,2},{2,3},{3,4},{4,5},{5,6},{6,7},{7,8},{8,9},{9,10},{10,1... | collective-permute-start | bytes 12296 | tf_op jit(solution)/shard_map/ppermute | solution.py:19
  164.1 7.7 %collective-permute-start.1 = (bf16[2,8,2,64]{0,3,1,2:T(8,128)(2,1)S(1)}, bf16[2,8,2,64]{0,3,1,2:T(8,128)(2,1)S(1)}, u32[]{:S(2)}, u32[]{:S(2)}) collective-permute-start(bf16[2,8,2,64]{0,3,1,2:T(8,128)(2,1)S(1)} %get-tuple-element.6), channel_id=1, source_target_pairs={{1,0},{2,1},{3,2},{4,3},{5,4},{6,5},{7,6},{8,7},{9,8},{10,9},{11,1... | collective-permute-start | bytes 12296 | tf_op jit(solution)/shard_map/ppermute | solution.py:20
  173.5 138.9 %copy-start.1 = (f32[16,31]{1,0:T(8,128)S(1)}, f32[16,31]{1,0:T(8,128)}, u32[]{:S(2)}) copy-start(f32[16,31]{1,0:T(8,128)} %param.10) | copy-start | bytes 5956
Sparse Core Ops, SparseCore 0:
  24.1 80.1 all-gather.1

commit v2 on v1

v2 whole, which is shorter than its diff:
```python
import functools
import math

import jax
import jax.numpy as jnp
from jax import lax
from jax.experimental import pallas as pl
from jax.experimental.pallas import tpu as pltpu
from jax.sharding import PartitionSpec as P

TAPS = 31
HALO = 2
LANES = 128


def ring_of(mesh):
    size = mesh.shape["surf"]
    chips = list(range(size // 2))
    row = mesh.devices.reshape(mesh.shape["group"], size)[0]
    try:
        places = [tuple(row[2 * chip].coords) for chip in chips]
    except AttributeError:
        return chips
    low = [min(place[d] for place in places) for d in range(3)]
    span = [max(place[d] for place in places) - low[d] + 1 for d in range(3)]
    dims = [d for d in range(3) if span[d] > 1]
    if len(dims) != 2 or span[dims[0]] * span[dims[1]] != len(chips):
        return chips
    a, b = dims if span[dims[0]] % 2 == 0 else dims[::-1]
    if span[a] % 2 or len(set(places)) != len(chips):
        return chips
    order = []
    for i in range(span[a]):
        across = range(1, span[b])
        order += [(i, j) for j in (across if i % 2 == 0 else reversed(across))]
    order += [(i, 0) for i in reversed(range(span[a]))]
    at = {(place[a] - low[a], place[b] - low[b]): chip for chip, place in zip(chips, places)}
    return [at[place] for place in order]


def spectra_kernel(freq_ref, traces_ref, out_ref, table_ref, turned_ref):
    points, shots, samples = traces_ref.shape
    freqs = out_ref.shape[0]
    parts = 2 * freqs

    @pl.when(pl.program_id(0) == 0)
    def _():
        time = lax.broadcasted_iota(jnp.int32, table_ref.shape, 0)
        lane = lax.broadcasted_iota(jnp.int32, table_ref.shape, 1)
        bins = jnp.zeros(table_ref.shape, jnp.int32)
        for f in range(freqs):
            bins = jnp.where(lane // 2 == f, freq_ref[f], bins)
        product = time * bins
        if samples & (samples - 1) == 0:
            phases = product & (samples - 1)
        else:
            phases = lax.rem(product, samples)
        angles = 2.0 * math.pi / samples * phases.astype(jnp.float32)
        table = jnp.where(lane % 2 == 0, jnp.cos(angles), -jnp.sin(angles))
        table_ref[...] = table.astype(jnp.bfloat16)

    rows = traces_ref[...].reshape(points * shots, samples)
    bands = jnp.dot(rows, table_ref[...], preferred_element_type=jnp.float32)
    together = LANES // shots
    for group in range(points // together):
        turned = bands[group * LANES : (group + 1) * LANES].T[:parts]
        for j in range(together):
            place = (group * together + j) * parts
            turned_ref[place : place + parts] = turned[:, j * shots : (j + 1) * shots]
    for f in range(freqs):
        real = turned_ref[pl.ds(2 * f, points, stride=parts), :]
        imag = turned_ref[pl.ds(2 * f + 1, points, stride=parts), :]
        out_ref[f] = jnp.concatenate([real, imag], axis=1).astype(jnp.bfloat16)


def spectra_of(traces, freq_bins, first, count):
    _, shots, samples = traces.shape
    freqs = freq_bins.shape[0]
    points = 16
    return pl.pallas_call(
        spectra_kernel,
        grid=(count // points,),
        in_specs=[
            pl.BlockSpec(memory_space=pltpu.SMEM),
            pl.BlockSpec((points, shots, samples), lambda i: (first // points + i, 0, 0)),
        ],
        out_specs=pl.BlockSpec((freqs, points, 2 * shots), lambda i: (0, i, 0)),
        out_shape=jax.ShapeDtypeStruct((freqs, count, 2 * shots), jnp.bfloat16),
        scratch_shapes=[
            pltpu.VMEM((samples, LANES), jnp.bfloat16),
            pltpu.VMEM((points * 2 * freqs, shots), jnp.float32),
        ],
        cost_estimate=pl.CostEstimate(
            flops=2 * count * shots * samples * LANES, bytes_accessed=count * shots * samples * 2, transcendentals=0
        ),
        name="spectra",
    )(freq_bins, traces)


def product_kernel(blocks_ref, swap_ref, op_ref, *refs, pairs, carried, final):
    refs = list(refs)
    pieces = [(refs.pop(0), refs.pop(0)) for _ in range(pairs)]
    carry_ref = refs.pop(0) if carried else None
    out_ref = refs.pop(0)
    acc_ref = refs.pop(0) if final else out_ref
    step = pl.program_id(0)
    receivers, freqs, _, width = op_ref.shape

    @pl.when(step == 0)
    def _():
        acc_ref[...] = carry_ref[...] if carried else jnp.zeros_like(acc_ref)

    swap = swap_ref[0] == 1
    for f in range(freqs):
        a, b = pieces[0][0][f], pieces[0][1][f]
        for i in range(1, pairs):
            a = jnp.where(step == i, pieces[i][0][f], a)
            b = jnp.where(step == i, pieces[i][1][f], b)
        both = jnp.concatenate([jnp.where(swap, b, a), jnp.where(swap, a, b)], axis=0)
        lhs = op_ref[:, f].reshape(2 * receivers, width)
        acc_ref[f] += jnp.dot(lhs, both, preferred_element_type=jnp.float32)

    if final:

        @pl.when(step == pl.num_programs(0) - 1)
        def _():
            combine(acc_ref, out_ref, receivers, freqs)


def combine(acc_ref, out_ref, receivers, freqs):
    width = acc_ref.shape[2]
    lane = lax.broadcasted_iota(jnp.int32, (receivers, width), 1)
    for f in range(freqs):
        with_real = acc_ref[f, pl.ds(0, receivers, stride=2), :]
        with_imag = acc_ref[f, pl.ds(1, receivers, stride=2), :]
        turned = pltpu.roll(with_imag, width // 2, 1)
        both = with_real + jnp.where(lane < width // 2, -turned, turned)
        out_ref[pl.ds(f, receivers, stride=freqs), :] = both


def product_cost(receivers, freqs, width, lanes):
    return pl.CostEstimate(
        flops=4 * receivers * freqs * width * lanes, bytes_accessed=4 * receivers * freqs * width, transcendentals=0
    )


def products_with(operator, blocks, swap, pairs, carry, final):
    receivers, freqs, _, _ = operator.shape
    points, lanes = pairs[0][0].shape[1:]
    whole = lambda *_: (0, 0, 0)
    shape = (freqs, 2 * receivers, lanes)
    acc = pl.BlockSpec(shape, whole)
    piece = pl.BlockSpec((freqs, points, lanes), whole)
    flat = [array for pair in pairs for array in pair]
    if final:
        out_shape = jax.ShapeDtypeStruct((receivers * freqs, lanes), jnp.float32)
        out_specs = pl.BlockSpec((receivers * freqs, lanes), lambda *_: (0, 0))
    else:
        out_shape, out_specs = jax.ShapeDtypeStruct(shape, jnp.float32), acc
    return pl.pallas_call(
        functools.partial(product_kernel, pairs=len(pairs), carried=carry is not None, final=final),
        grid_spec=pltpu.PrefetchScalarGridSpec(
            num_scalar_prefetch=2,
            grid=(len(pairs),),
            in_specs=[pl.BlockSpec((receivers, freqs, 2, 2 * points), lambda i, at, _: (0, 0, 0, at[i]))]
            + [piece] * len(flat)
            + ([acc] if carry is not None else []),
            out_specs=out_specs,
            scratch_shapes=[pltpu.VMEM(shape, jnp.float32)] if final else [],
        ),
        out_shape=out_shape,
        input_output_aliases={3 + len(flat): 0} if carry is not None and not final else {},
        cost_estimate=product_cost(receivers, freqs, 2 * points * len(pairs), lanes),
        name="product",
    )(blocks, swap, operator, *flat, *([carry] if carry is not None else []))


def whole_product_kernel(op_ref, spectra_ref, out_ref, acc_ref):
    step = pl.program_id(0)
    receivers, freqs, _, width = op_ref.shape

    @pl.when(step == 0)
    def _():
        acc_ref[...] = jnp.zeros_like(acc_ref)

    for f in range(freqs):
        lhs = op_ref[:, f].reshape(2 * receivers, width)
        acc_ref[f] += jnp.dot(lhs, spectra_ref[f], preferred_element_type=jnp.float32)

    @pl.when(step == pl.num_programs(0) - 1)
    def _():
        combine(acc_ref, out_ref, receivers, freqs)


def whole_product(operator, spectra):
    receivers, freqs, _, sources = operator.shape
    lanes = spectra.shape[2]
    width = 4 * LANES
    return pl.pallas_call(
        whole_product_kernel,
        grid=(sources // width,),
        in_specs=[
            pl.BlockSpec((receivers, freqs, 2, width), lambda i: (0, 0, 0, i)),
            pl.BlockSpec((freqs, width, lanes), lambda i: (0, i, 0)),
        ],
        out_specs=pl.BlockSpec((receivers * freqs, lanes), lambda i: (0, 0)),
        out_shape=jax.ShapeDtypeStruct((receivers * freqs, lanes), jnp.float32),
        scratch_shapes=[pltpu.VMEM((freqs, 2 * receivers, lanes), jnp.float32)],
        cost_estimate=product_cost(receivers, freqs, sources, lanes),
        name="whole_product",
    )(operator, spectra)


def subtract_points(offset_of, pred_ref, shift, base, basis_ref, traces_ref, out_ref):
    points, shots, samples = traces_ref.shape
    lanes = pred_ref.shape[2]
    lane = lax.broadcasted_iota(jnp.int32, pred_ref.shape[1:], 1)
    low = lane < lanes // 2
    columns = []
    for p in range(0, points, 2):
        mixed = []
        for q in (p, p + 1):
            here = pred_ref[base + q + shift]
            there = pred_ref[base + q + shift + offset_of(q)]
            mixed.append(here + 0.5 * there)
        first, second = mixed
        real = jnp.where(low, first, pltpu.roll(second, lanes // 2, 1))
        imag = jnp.where(low, pltpu.roll(first, lanes // 2, 1), second)
        columns.append(jnp.concatenate([real, imag], axis=0))
    rows = jnp.concatenate(columns, axis=1)
    high = rows.astype(jnp.bfloat16)
    rest = (rows - high.astype(jnp.float32)).astype(jnp.bfloat16)
    left = jnp.concatenate([high, rest, high], axis=0)
    adapted = lax.dot_general(left, basis_ref[...], (((0,), (0,)), ((), ())), preferred_element_type=jnp.float32)
    traces = traces_ref[...].reshape(points * shots, samples).astype(jnp.float32)
    out_ref[...] = (traces - adapted).astype(jnp.bfloat16).reshape(points, shots, samples)


def inner_kernel(offset_ref, pred_ref, basis_ref, traces_ref, out_ref):
    points = traces_ref.shape[0]
    base = (pl.program_id(0) + 1) * points
    subtract_points(lambda q: offset_ref[base + q], pred_ref, 0, base, basis_ref, traces_ref, out_ref)


def edge_kernel(offset_ref, pred_ref, before_ref, after_ref, basis_ref, traces_ref, given_ref, out_ref, near_ref):
    points = traces_ref.shape[0]
    receivers = pred_ref.shape[0]
    step = pl.program_id(0)

    @pl.when(step == 0)
    def _():
        near_ref[:HALO] = before_ref[...]
        near_ref[HALO:] = pred_ref[: points + HALO]

    @pl.when(step == 1)
    def _():
        near_ref[: points + HALO] = pred_ref[receivers - points - HALO :]
        near_ref[points + HALO :] = after_ref[...]

    base = step * (receivers - points)
    subtract_points(lambda q: offset_ref[base + q], near_ref, HALO, 0, basis_ref, traces_ref, out_ref)


def subtract(traces, predicted, neighbour, basis):
    receivers, shots, samples = traces.shape
    freqs, lanes = predicted.shape[1:]
    points = 8
    blocks = receivers // points
    smem = pl.BlockSpec(memory_space=pltpu.SMEM)
    vmem = pl.BlockSpec(memory_space=pltpu.VMEM)
    out_shape = jax.ShapeDtypeStruct(traces.shape, traces.dtype)
    cost = lambda n: pl.CostEstimate(
        flops=2 * n * points * shots * samples * 48, bytes_accessed=4 * n * points * shots * samples, transcendentals=0
    )
    inner = pl.BlockSpec((points, shots, samples), lambda i: (i + 1, 0, 0))
    central = pl.pallas_call(
        inner_kernel,
        grid=(blocks - 2,),
        in_specs=[smem, vmem, vmem, inner],
        out_specs=inner,
        out_shape=out_shape,
        cost_estimate=cost(blocks - 2),
        name="inner",
    )(neighbour, predicted, basis, traces)
    size = lax.axis_size("surf")
    up = [(i, i + 1) for i in range(size - 1)]
    before = lax.ppermute(predicted[receivers - HALO :], "surf", up)
    after = lax.ppermute(predicted[:HALO], "surf", [(j, i) for i, j in up])
    edge = pl.BlockSpec((points, shots, samples), lambda i: (i * (blocks - 1), 0, 0))
    return pl.pallas_call(
        edge_kernel,
        grid=(2,),
        in_specs=[smem, vmem, vmem, vmem, vmem, edge, pl.BlockSpec(memory_space=pl.ANY)],
        out_specs=edge,
        out_shape=out_shape,
        scratch_shapes=[pltpu.VMEM((points + 2 * HALO, freqs, lanes), jnp.float32)],
        input_output_aliases={6: 0},
        cost_estimate=cost(2),
        name="edge",
    )(neighbour, predicted, before, after, basis, traces, central)


def matching(series, coefficients, win_lengths):
    samples = series.shape[1]
    half_taps = (TAPS - 1) // 2
    window_ends = jnp.cumsum(win_lengths)
    sample_index = jnp.arange(samples, dtype=jnp.int32)
    window = jnp.sum((window_ends[None, :] <= sample_index[:, None]).astype(jnp.int32), axis=1)
    membership = (
        window[:, None] == jnp.arange(coefficients.shape[0], dtype=jnp.int32)[None, :]
    ).astype(jnp.float32)
    per_sample = jnp.dot(membership, coefficients, precision=lax.Precision.HIGHEST)
    padded = jnp.pad(series, ((0, 0), (half_taps, half_taps)))
    summed = jnp.zeros_like(series)
    for lag_index in range(TAPS):
        summed = summed + per_sample[:, lag_index] * padded[:, lag_index : lag_index + samples]
    return summed


def basis_of(freq_bins, win_lengths, coefficients, samples):
    freqs = freq_bins.shape[0]
    sample_index = jnp.arange(samples, dtype=jnp.int32)
    phases = freq_bins[:, None] * sample_index[None, :] % samples
    angles = 2.0 * math.pi / samples * phases.astype(jnp.float32)
    norm_divisor = (2.0 * freqs * samples) ** (-0.5)
    waves = norm_divisor * jnp.concatenate([jnp.cos(angles), -jnp.sin(angles)], axis=0)
    basis = matching(waves, coefficients, win_lengths)
    high = lax.reduce_precision(basis, 8, 7)
    high16, rest16 = high.astype(jnp.bfloat16), (basis - high).astype(jnp.bfloat16)
    return jnp.concatenate([high16, high16, rest16], axis=0)


def predict_in_ring(ring, operator, own):
    size = lax.axis_size("surf")
    chips = size // 2
    ahead = []
    for i, chip in enumerate(ring):
        ahead.append((2 * chip, 2 * ring[(i + 1) % chips]))
        ahead.append((2 * chip + 1, 2 * ring[(i - 1) % chips] + 1))
    across = [(i, i ^ 1) for i in range(size)]
    step_ring = lambda x: lax.ppermute(x, "surf", ahead)
    step_chip = lambda x: lax.ppermute(x, "surf", across)

    me = lax.axis_index("surf")
    core = me % 2
    order = jnp.asarray(ring, jnp.int32)
    position = jnp.argmax(order == me // 2).astype(jnp.int32)
    away = jnp.where(core == 0, -1, 1)
    chip_at = lambda hops: order[(position + away * hops + chips) % chips]
    same = core.astype(jnp.int32)[None]

    half = chips // 2
    u, w = own, step_chip(own)
    carry = None
    pending = ([chip_at(0)], [(u, w)])
    for k in range(1, half):
        u_next, w_next = step_ring(u), step_ring(w)
        carry = products_with(operator, jnp.stack(pending[0]), same, pending[1], carry, False)
        u, w = u_next, w_next
        v, x = step_chip(u), step_chip(w)
        pending = ([chip_at(k), chip_at(-k)], [(u, w), (x, v)])
    u = step_ring(u)
    carry = products_with(operator, jnp.stack(pending[0]), same, pending[1], carry, False)
    v = step_chip(u)
    return products_with(operator, chip_at(half)[None], same, [(u, v)], carry, True)


def on_device(ring, traces, operator, freq_bins, win_lengths, coefficients, neighbour):
    points, shots, samples = traces.shape
    freqs = freq_bins.shape[0]
    own = spectra_of(traces, freq_bins, 0, points)
    if 2 * points % LANES == 0 and len(ring) % 2 == 0 and len(ring) <= 8:
        predicted = predict_in_ring(ring, operator, own)
    else:
        gathered = lax.all_gather(own, "surf", axis=1, tiled=True)
        predicted = whole_product(operator, gathered)
    predicted = predicted.reshape(points, freqs, 2 * shots)
    basis = basis_of(freq_bins, win_lengths, coefficients, samples)
    return subtract(traces, predicted, neighbour, basis)


def solution(mesh):
    return jax.shard_map(
        functools.partial(on_device, ring_of(mesh)),
        mesh=mesh,
        in_specs=(P("surf", "group", None), P("surf", None, None, None), P(), P(), P(), P("surf")),
        out_specs=P("surf", "group", None),
        check_vma=False,
    )
```

time: 319 us -> 162 us (0.51)
  matrix products: 179 us -> 0.52 us
  Pallas kernels: 0 us -> 104 us
  waiting for transfers between devices: 84.7 us -> 19.4 us
  local copies, waits for them, and re-layouts: 33.6 us -> 2.74 us
  starting transfers between devices: 5.14 us -> 20.3 us
  between operations: 13.6 us -> 5.39 us
  other arithmetic: 3.32 us -> 7.86 us
    dot_general x3 -> x0, matrix products: 178 us -> none  [the longest x1 108 us: to_traces(): timed = jnp.dot(rows, basis, precision=lax.Precision.HIGHEST)]
    pallas_call x0 -> x8, Pallas kernels: none -> 104 us  [the longest x1 38.3 us: subtract(): pl.pallas_call(inner_kernel, grid=(blocks - 2,), in_specs=[smem, vmem, vm...]
    all_gather x1 -> x0, waiting for transfers between devices: 79 us -> none  [on_device(): gathered = lax.all_gather(spectra, 'surf', axis=0, tiled=True)]
    convert_element_type x2 -> x0, local copies, waits for them, and re-layouts: 30.8 us -> none  [the longest x1 30.8 us: on_device(): return (traces.astype(jnp.float32) - adapted).astype(jnp.bfloat16)]
    ppermute x2 -> x17, starting transfers between devices: 5.14 us -> 20.3 us  [the longest x7 11.1 us: predict_in_ring(): step_ring = lambda x: lax.ppermute(x, 'surf', ahead)]
    ppermute x2 -> x17, waiting for transfers between devices: 5.74 us -> 19.4 us  [the longest x7 19.4 us: predict_in_ring(): step_ring = lambda x: lax.ppermute(x, 'surf', ahead)]
    another operation x5 -> x6, other arithmetic: 1.1 us -> 6.27 us  [the longest x3 5.44 us: predict_in_ring(): jnp.stack(pending[0])]
  transfers between devices with their start and end apart: 3 -> 17, of which waited for: 3 -> 5; matrix products, arithmetic and copies ran while one was open for 0% -> 6% of each run, Pallas kernels for 0% -> 43%
where the time goes in v2:
time: 162 us; the launch traced here: 160 us
  Pallas kernels  104 us (64%)
  starting transfers between devices  20.3 us (13%)
  waiting for transfers between devices  19.4 us (12%)
  other arithmetic  7.86 us (5%)
  between operations  5.39 us (3%)
  local copies, waits for them, and re-layouts  2.74 us (2%)
    pallas_call x1, Pallas kernels, subtract(): pl.pallas_call(inner_kernel, grid=(blocks - 2,), in_specs=[smem, vmem, vm...  38.3 us
    pallas_call x5, Pallas kernels, products_with(): pl.pallas_call(functools.partial(product_kernel, pairs=len(pairs), carrie...  37.3 us
    pallas_call x1, Pallas kernels, spectra_of(): pl.pallas_call(spectra_kernel, grid=(count // points,), in_specs=[pl.Bloc...  24.8 us
    ppermute x7, waiting for transfers between devices, predict_in_ring(): step_ring = lambda x: lax.ppermute(x, 'surf', ahead)  19.4 us
    ppermute x7, starting transfers between devices, predict_in_ring(): step_ring = lambda x: lax.ppermute(x, 'surf', ahead)  11.1 us
    another operation x3, other arithmetic, predict_in_ring(): jnp.stack(pending[0])  5.44 us
    pallas_call x1, Pallas kernels, subtract(): pl.pallas_call(edge_kernel, grid=(2,), in_specs=[smem, vmem, vmem, vmem,...  3.67 us
    ppermute x8, starting transfers between devices, predict_in_ring(): step_chip = lambda x: lax.ppermute(x, 'surf', across)  3.63 us
  transfers between devices with their start and end apart: 17, of which 5 were waited for; matrix products, arithmetic and copies ran while one was open for 6% of the time, Pallas kernels for 43%

profile of v2, /device:TPU:1, one launch (start us, length us, event | category | flops | bytes accessed | tf_op | source)
XLA Modules:
  0.0 160.3 jit_solution(4517789955082168532)
XLA Ops:
  0.0 0.0 copy-start
  0.0 0.0 copy-start.12
  0.0 24.8 %spectra.1.refs_0_ = bf16[8,256,128]{2,1,0:T(8,128)(2,1)} custom-call(s32[8]{0:T(128)} %freq_ref.1, bf16[256,64,1024]{2,1,0:T(8,128)(2,1)} %traces_ref.5), custom_call_target="tpu_custom_call" | custom-call | flops 4294967296 | bytes 33554432 | tf_op jit(solution)/shard_map/spectra/pallas_call | solution.py:80
  24.8 0.0 collective-permute-start.5
  24.8 2.7 %collective-permute-start = (bf16[8,256,128]{2,1,0:T(8,128)(2,1)}, bf16[8,256,128]{2,1,0:T(8,128)(2,1)S(1)}, u32[]{:S(2)}, u32[]{:S(2)}) collective-permute-start(bf16[8,256,128]{2,1,0:T(8,128)(2,1)} %spectra.1.refs_0_), channel_id=1, source_target_pairs={{4,8},{5,1},{8,12},{9,5},{12,14},{13,9},{14,10},{15,13},{10,6},{11... | collective-permute-start | bytes 1572872 | tf_op jit(solution)/shard_map/ppermute | solution.py:341
  27.5 0.1 copy.14
  27.6 0.1 reduce.18
  27.8 0.0 copy-done.11
  27.8 0.2 fusion.70
  28.0 0.0 collective-permute-done.5.refs_1_
  28.0 1.3 collective-permute-start.6
  29.4 5.3 %collective-permute-done.refs_0_ = bf16[8,256,128]{2,1,0:T(8,128)(2,1)S(1)} collective-permute-done((bf16[8,256,128]{2,1,0:T(8,128)(2,1)}, bf16[8,256,128]{2,1,0:T(8,128)(2,1)S(1)}, u32[]{:S(2)}, u32[]{:S(2)}) %collective-permute-start) | collective-permute-done | bytes 524320 | tf_op jit(solution)/shard_map/ppermute | solution.py:341
  34.7 1.4 collective-permute-start.1
  36.1 0.1 convert_reduce_fusion
  36.2 0.5 fusion
  36.7 3.5 %collective-permute-done.6.refs_1_ = bf16[8,256,128]{2,1,0:T(8,128)(2,1)S(1)} collective-permute-done((bf16[8,256,128]{2,1,0:T(8,128)(2,1)S(1)}, bf16[8,256,128]{2,1,0:T(8,128)(2,1)S(1)}, u32[]{:S(2)}, u32[]{:S(2)}) %collective-permute-start.6) | collective-permute-done | bytes 524320 | tf_op jit(solution)/shard_map/ppermute | solution.py:341
  40.3 1.4 collective-permute-start.7
  41.7 4.2 %collective-permute-done.1.refs_0_ = bf16[8,256,128]{2,1,0:T(8,128)(2,1)S(1)} collective-permute-done((bf16[8,256,128]{2,1,0:T(8,128)(2,1)S(1)}, bf16[8,256,128]{2,1,0:T(8,128)(2,1)S(1)}, u32[]{:S(2)}, u32[]{:S(2)}) %collective-permute-start.1) | collective-permute-done | bytes 524320 | tf_op jit(solution)/shard_map/ppermute | solution.py:341
  45.9 1.4 collective-permute-start.2
  47.3 0.1 fusion.72
  47.4 1.3 collective-permute-start.14
  48.6 0.6 reduce-precision_convert_fusion
  49.2 0.1 collective-permute-start.13
  49.3 2.2 %collective-permute-done.7.refs_1_ = bf16[8,256,128]{2,1,0:T(8,128)(2,1)S(1)} collective-permute-done((bf16[8,256,128]{2,1,0:T(8,128)(2,1)S(1)}, bf16[8,256,128]{2,1,0:T(8,128)(2,1)S(1)}, u32[]{:S(2)}, u32[]{:S(2)}) %collective-permute-start.7) | collective-permute-done | bytes 524320 | tf_op jit(solution)/shard_map/ppermute | solution.py:341
  51.5 1.4 collective-permute-start.8
  52.9 4.2 %collective-permute-done.2.refs_0_ = bf16[8,256,128]{2,1,0:T(8,128)(2,1)S(1)} collective-permute-done((bf16[8,256,128]{2,1,0:T(8,128)(2,1)S(1)}, bf16[8,256,128]{2,1,0:T(8,128)(2,1)S(1)}, u32[]{:S(2)}, u32[]{:S(2)}) %collective-permute-start.2) | collective-permute-done | bytes 524320 | tf_op jit(solution)/shard_map/ppermute | solution.py:341
  57.1 1.4 collective-permute-start.3
  58.5 0.7 compare_reduce_fusion
  64.4 0.7 fusion.74
  65.1 1.3 collective-permute-start.12
  66.4 0.0 collective-permute-done.14.refs_3_
  66.4 0.1 collective-permute-start.11
  66.5 1.9 %pad_add_fusion.2.blocks_ref = s32[2]{0:T(128)} fusion(s32[1]{0:T(128)} %get-tuple-element.51, s32[1]{0:T(128)} %get-tuple-element.45), kind=kLoop, calls=%fused_computation.118 | loop fusion | flops 2 | bytes 16 | tf_op jit(solution)/shard_map/stack | solution.py:358
  68.4 0.0 collective-permute-done.13.refs_2_
  68.4 0.4 collective-permute-start.10
  68.8 0.0 collective-permute-done.8.refs_1_
  68.8 0.1 collective-permute-start.9
  68.9 1.7 %pad_add_fusion.1.blocks_ref = s32[2]{0:T(128)} fusion(s32[1]{0:T(128)} %get-tuple-element.46, s32[1]{0:T(128)} %get-tuple-element.47), kind=kLoop, calls=%fused_computation.117 | loop fusion | flops 2 | bytes 16 | tf_op jit(solution)/shard_map/stack | solution.py:358
  70.7 0.0 collective-permute-done.3.refs_0_
  70.7 0.4 collective-permute-start.4
  71.1 1.8 %pad_add_fusion.blocks_ref = s32[2]{0:T(128)} fusion(s32[1]{0:T(128)} %get-tuple-element.48, s32[1]{0:T(128)} %get-tuple-element.49), kind=kLoop, calls=%fused_computation.116 | loop fusion | flops 2 | bytes 16 | tf_op jit(solution)/shard_map/stack | solution.py:363
  72.9 0.6 pad_maximum_fusion.basis_ref
  73.5 5.7 %product.5.refs_4_ = f32[8,512,128]{2,1,0:T(8,128)} custom-call(s32[1]{0:T(128)} %get-tuple-element.44.blocks_ref, s32[1]{0:T(128)} %bitcast.swap_ref, bf16[256,8,2,4096]{3,2,1,0:T(2,128)(2,1)} %op_ref.9, bf16[8,256,128]{2,1,0:T(8,128)(2,1)} %spectra.1.refs_0_, bf16[8,256,128]{2,1,0:T(8,128)(2,1)} %copy-done.2), custom_call_target="tpu_custom_call" | custom-call | flops 536870912 | bytes 4194304 | tf_op jit(solution)/shard_map/product/pallas_call | solution.py:160
  79.2 0.0 copy-done.3
  79.2 8.3 %product.6.refs_4_ = f32[8,512,128]{2,1,0:T(8,128)} custom-call(s32[2]{0:T(128)} %pad_add_fusion.2.blocks_ref, s32[1]{0:T(128)} %bitcast.swap_ref, bf16[256,8,2,4096]{3,2,1,0:T(2,128)(2,1)} %op_ref.9, bf16[8,256,128]{2,1,0:T(8,128)(2,1)} %copy-done.3, bf16[8,256,128]{2,1,0:T(8,128)(2,1)} %copy-done.5, ...), custom_call_target="tpu_custom_call", output_to_operand_aliasing={{}: (7, {})} | custom-call | flops 1073741824 | bytes 8388608 | tf_op jit(solution)/shard_map/product/pallas_call | solution.py:160
  87.6 0.0 copy-done.4
  87.6 0.0 collective-permute-done.12.refs_3_
  87.6 0.0 collective-permute-done.11.refs_2_
  87.6 8.4 %product.7.refs_4_ = f32[8,512,128]{2,1,0:T(8,128)} custom-call(s32[2]{0:T(128)} %pad_add_fusion.1.blocks_ref, s32[1]{0:T(128)} %bitcast.swap_ref, bf16[256,8,2,4096]{3,2,1,0:T(2,128)(2,1)} %op_ref.9, bf16[8,256,128]{2,1,0:T(8,128)(2,1)} %copy-done.4, bf16[8,256,128]{2,1,0:T(8,128)(2,1)} %copy-done.7, ...), custom_call_target="tpu_custom_call", output_to_operand_aliasing={{}: (7, {})} | custom-call | flops 1073741824 | bytes 8388608 | tf_op jit(solution)/shard_map/product/pallas_call | solution.py:160
  96.0 0.0 collective-permute-done.10.refs_3_
  96.0 0.0 collective-permute-done.9.refs_2_
  96.0 8.4 %product.8.refs_2_ = f32[8,512,128]{2,1,0:T(8,128)} custom-call(s32[2]{0:T(128)} %pad_add_fusion.blocks_ref, s32[1]{0:T(128)} %bitcast.swap_ref, bf16[256,8,2,4096]{3,2,1,0:T(2,128)(2,1)} %op_ref.9, bf16[8,256,128]{2,1,0:T(8,128)(2,1)} %copy-done.6, bf16[8,256,128]{2,1,0:T(8,128)(2,1)} %collective-permute-done.8.refs_1_, ...), custom_call_target="tpu_custom_call", output_to_operand_aliasing={{}: (7, {})} | custom-call | flops 1073741824 | bytes 8388608 | tf_op jit(solution)/shard_map/product/pallas_call | solution.py:160
  104.3 0.0 collective-permute-done.4.refs_1_
  104.3 6.5 %product.9 = f32[2048,128]{1,0:T(8,128)} custom-call(s32[1]{0:T(128)} %get-tuple-element.50.blocks_ref, s32[1]{0:T(128)} %bitcast.swap_ref, bf16[256,8,2,4096]{3,2,1,0:T(2,128)(2,1)} %op_ref.9, bf16[8,256,128]{2,1,0:T(8,128)(2,1)} %collective-permute-done.3.refs_0_, bf16[8,256,128]{2,1,0:T(8,128)(2,1)} %collective-permute-done.4.refs_1_, ...), custom_call_target="tpu_custom_call" | custom-call | flops 536870912 | bytes 4194304 | tf_op jit(solution)/shard_map/product/pallas_call | solution.py:160
  110.9 0.7 slice_bitcast_fusion
  111.6 2.0 %collective-permute-start.16 = (f32[2,8,128]{2,1,0:T(8,128)S(1)}, f32[2,8,128]{2,1,0:T(8,128)S(1)}, u32[]{:S(2)}, u32[]{:S(2)}) collective-permute-start(f32[2,8,128]{2,1,0:T(8,128)S(1)} %get-tuple-element.9), channel_id=1, source_target_pairs={{1,0},{2,1},{3,2},{4,3},{5,4},{6,5},{7,6},{8,7},{9,8},{10,9},{11,1... | collective-permute-start | bytes 24584 | tf_op jit(solution)/shard_map/ppermute | solution.py:288
  113.6 3.6 %collective-permute-start.15 = (f32[2,8,128]{2,1,0:T(8,128)S(1)}, f32[2,8,128]{2,1,0:T(8,128)S(1)}, u32[]{:S(2)}, u32[]{:S(2)}) collective-permute-start(f32[2,8,128]{2,1,0:T(8,128)S(1)} %get-tuple-element.10), channel_id=1, source_target_pairs={{0,1},{1,2},{2,3},{3,4},{4,5},{5,6},{6,7},{7,8},{8,9},{9,10},{10,1... | collective-permute-start | bytes 24584 | tf_op jit(solution)/shard_map/ppermute | solution.py:287
  117.1 0.0 copy-start.1
  117.2 38.3 %inner.1.given_ref = bf16[256,64,1024]{2,1,0:T(8,128)(2,1)} custom-call(s32[256]{0:T(256)} %offset_ref.3, f32[256,8,128]{2,1,0:T(8,128)} %bitcast.39, bf16[48,1024]{1,0:T(8,128)(2,1)} %pad_maximum_fusion.basis_ref, bf16[256,64,1024]{2,1,0:T(8,128)(2,1)} %traces_ref.5), custom_call_target="tpu_custom_call" | custom-call | flops 1509949440 | bytes 62914560 | tf_op jit(solution)/shard_map/inner/pallas_call | solution.py:276
  155.5 0.0 collective-permute-done.16.after_ref
  155.5 0.0 collective-permute-done.15.before_ref
  155.5 0.6 copy-done.9
  156.1 0.6 copy-done.10
  156.7 3.7 %edge.1 = bf16[256,64,1024]{2,1,0:T(8,128)(2,1)} custom-call(s32[256]{0:T(256)} %offset_ref.3, f32[256,8,128]{2,1,0:T(8,128)} %bitcast.40, f32[2,8,128]{2,1,0:T(8,128)} %copy-done.10, f32[2,8,128]{2,1,0:T(8,128)} %copy-done.9, bf16[48,1024]{1,0:T(8,128)(2,1)} %pad_maximum_fusion.basis_ref, ...), custom_call_target="tpu_custom_call", output_to_operand_aliasing={{}: (6, {})} | custom-call | flops 100663296 | bytes 4194304 | tf_op jit(solution)/shard_map/edge/pallas_call | solution.py:290
  (22 shorter events, 0.1 us)
Async XLA Ops:
  0.0 36.2 %copy-start = (f32[16,31]{1,0:T(8,128)S(1)}, f32[16,31]{1,0:T(8,128)}, u32[]{:S(2)}) copy-start(f32[16,31]{1,0:T(8,128)} %param.11) | copy-start | bytes 5956
  0.0 58.5 %copy-start.8 = (s32[8]{0:T(128)S(1)}, s32[8]{0:T(128)}, u32[]{:S(2)}) copy-start(s32[8]{0:T(128)} %constant.107.clone) | copy-start | bytes 100
  0.0 27.8 %copy-start.11 = (s32[8]{0:T(128)S(1)}, s32[8]{0:T(128)}, u32[]{:S(2)}) copy-start(s32[8]{0:T(128)} %freq_ref.1) | copy-start | bytes 100
  0.0 27.5 %copy-start.12 = (s32[16]{0:T(128)S(1)}, s32[16]{0:T(128)}, u32[]{:S(2)}) copy-start(s32[16]{0:T(128)} %param.10) | copy-start | bytes 196
  24.8 3.2 %collective-permute-start.5 = (bf16[8,256,128]{2,1,0:T(8,128)(2,1)}, bf16[8,256,128]{2,1,0:T(8,128)(2,1)S(1)}, u32[]{:S(2)}, u32[]{:S(2)}) collective-permute-start(bf16[8,256,128]{2,1,0:T(8,128)(2,1)} %spectra.1.refs_0_), channel_id=1, source_target_pairs={{0,1},{1,0},{2,3},{3,2},{4,5},{5,4},{6,7},{7,6},{8,9},{9,8},{10,11... | collective-permute-start | bytes 1572872 | tf_op jit(solution)/shard_map/ppermute | solution.py:342
  24.8 9.9 %collective-permute-start = (bf16[8,256,128]{2,1,0:T(8,128)(2,1)}, bf16[8,256,128]{2,1,0:T(8,128)(2,1)S(1)}, u32[]{:S(2)}, u32[]{:S(2)}) collective-permute-start(bf16[8,256,128]{2,1,0:T(8,128)(2,1)} %spectra.1.refs_0_), channel_id=1, source_target_pairs={{4,8},{5,1},{8,12},{9,5},{12,14},{13,9},{14,10},{15,13},{10,6},{11... | collective-permute-start | bytes 1572872 | tf_op jit(solution)/shard_map/ppermute | solution.py:341
  28.0 45.5 %copy-start.2 = (bf16[8,256,128]{2,1,0:T(8,128)(2,1)}, bf16[8,256,128]{2,1,0:T(8,128)(2,1)S(1)}, u32[]{:S(2)}) copy-start(bf16[8,256,128]{2,1,0:T(8,128)(2,1)S(1)} %collective-permute-done.5.refs_1_) | copy-start | bytes 1572868
  28.0 12.3 %collective-permute-start.6 = (bf16[8,256,128]{2,1,0:T(8,128)(2,1)S(1)}, bf16[8,256,128]{2,1,0:T(8,128)(2,1)S(1)}, u32[]{:S(2)}, u32[]{:S(2)}) collective-permute-start(bf16[8,256,128]{2,1,0:T(8,128)(2,1)S(1)} %collective-permute-done.5.refs_1_), channel_id=1, source_target_pairs={{4,8},{5,1},{8,12},{9,5},{12,14},{13,9},{14,10},{15,13},{10,6},{11... | collective-permute-start | bytes 1572872 | tf_op jit(solution)/shard_map/ppermute | solution.py:341
  34.6 44.6 %copy-start.3 = (bf16[8,256,128]{2,1,0:T(8,128)(2,1)}, bf16[8,256,128]{2,1,0:T(8,128)(2,1)S(1)}, u32[]{:S(2)}) copy-start(bf16[8,256,128]{2,1,0:T(8,128)(2,1)S(1)} %collective-permute-done.refs_0_) | copy-start | bytes 1572868
  34.7 11.2 %collective-permute-start.1 = (bf16[8,256,128]{2,1,0:T(8,128)(2,1)S(1)}, bf16[8,256,128]{2,1,0:T(8,128)(2,1)S(1)}, u32[]{:S(2)}, u32[]{:S(2)}) collective-permute-start(bf16[8,256,128]{2,1,0:T(8,128)(2,1)S(1)} %collective-permute-done.refs_0_), channel_id=1, source_target_pairs={{4,8},{5,1},{8,12},{9,5},{12,14},{13,9},{14,10},{15,13},{10,6},{11... | collective-permute-start | bytes 1572872 | tf_op jit(solution)/shard_map/ppermute | solution.py:341
  40.3 39.0 %copy-start.5 = (bf16[8,256,128]{2,1,0:T(8,128)(2,1)}, bf16[8,256,128]{2,1,0:T(8,128)(2,1)S(1)}, u32[]{:S(2)}) copy-start(bf16[8,256,128]{2,1,0:T(8,128)(2,1)S(1)} %collective-permute-done.6.refs_1_) | copy-start | bytes 1572868
  40.3 11.2 %collective-permute-start.7 = (bf16[8,256,128]{2,1,0:T(8,128)(2,1)S(1)}, bf16[8,256,128]{2,1,0:T(8,128)(2,1)S(1)}, u32[]{:S(2)}, u32[]{:S(2)}) collective-permute-start(bf16[8,256,128]{2,1,0:T(8,128)(2,1)S(1)} %collective-permute-done.6.refs_1_), channel_id=1, source_target_pairs={{4,8},{5,1},{8,12},{9,5},{12,14},{13,9},{14,10},{15,13},{10,6},{11... | collective-permute-start | bytes 1572872 | tf_op jit(solution)/shard_map/ppermute | solution.py:341
  45.9 41.7 %copy-start.4 = (bf16[8,256,128]{2,1,0:T(8,128)(2,1)}, bf16[8,256,128]{2,1,0:T(8,128)(2,1)S(1)}, u32[]{:S(2)}) copy-start(bf16[8,256,128]{2,1,0:T(8,128)(2,1)S(1)} %collective-permute-done.1.refs_0_) | copy-start | bytes 1572868
  45.9 11.2 %collective-permute-start.2 = (bf16[8,256,128]{2,1,0:T(8,128)(2,1)S(1)}, bf16[8,256,128]{2,1,0:T(8,128)(2,1)S(1)}, u32[]{:S(2)}, u32[]{:S(2)}) collective-permute-start(bf16[8,256,128]{2,1,0:T(8,128)(2,1)S(1)} %collective-permute-done.1.refs_0_), channel_id=1, source_target_pairs={{4,8},{5,1},{8,12},{9,5},{12,14},{13,9},{14,10},{15,13},{10,6},{11... | collective-permute-start | bytes 1572872 | tf_op jit(solution)/shard_map/ppermute | solution.py:341
  47.4 19.0 %collective-permute-start.14 = (bf16[8,256,128]{2,1,0:T(8,128)(2,1)S(1)}, bf16[8,256,128]{2,1,0:T(8,128)(2,1)}, u32[]{:S(2)}, u32[]{:S(2)}) collective-permute-start(bf16[8,256,128]{2,1,0:T(8,128)(2,1)S(1)} %collective-permute-done.refs_0_), channel_id=1, source_target_pairs={{0,1},{1,0},{2,3},{3,2},{4,5},{5,4},{6,7},{7,6},{8,9},{9,8},{10,11... | collective-permute-start | bytes 1572872 | tf_op jit(solution)/shard_map/ppermute | solution.py:342
  49.2 19.2 %collective-permute-start.13 = (bf16[8,256,128]{2,1,0:T(8,128)(2,1)S(1)}, bf16[8,256,128]{2,1,0:T(8,128)(2,1)}, u32[]{:S(2)}, u32[]{:S(2)}) collective-permute-start(bf16[8,256,128]{2,1,0:T(8,128)(2,1)S(1)} %collective-permute-done.6.refs_1_), channel_id=1, source_target_pairs={{0,1},{1,0},{2,3},{3,2},{4,5},{5,4},{6,7},{7,6},{8,9},{9,8},{10,11... | collective-permute-start | bytes 1572872 | tf_op jit(solution)/shard_map/ppermute | solution.py:342
  51.5 36.1 %copy-start.7 = (bf16[8,256,128]{2,1,0:T(8,128)(2,1)}, bf16[8,256,128]{2,1,0:T(8,128)(2,1)S(1)}, u32[]{:S(2)}) copy-start(bf16[8,256,128]{2,1,0:T(8,128)(2,1)S(1)} %collective-permute-done.7.refs_1_) | copy-start | bytes 1572868
  51.5 17.3 %collective-permute-start.8 = (bf16[8,256,128]{2,1,0:T(8,128)(2,1)S(1)}, bf16[8,256,128]{2,1,0:T(8,128)(2,1)}, u32[]{:S(2)}, u32[]{:S(2)}) collective-permute-start(bf16[8,256,128]{2,1,0:T(8,128)(2,1)S(1)} %collective-permute-done.7.refs_1_), channel_id=1, source_target_pairs={{4,8},{5,1},{8,12},{9,5},{12,14},{13,9},{14,10},{15,13},{10,6},{11... | collective-permute-start | bytes 1572872 | tf_op jit(solution)/shard_map/ppermute | solution.py:341
  57.1 30.5 %copy-start.6 = (bf16[8,256,128]{2,1,0:T(8,128)(2,1)}, bf16[8,256,128]{2,1,0:T(8,128)(2,1)S(1)}, u32[]{:S(2)}) copy-start(bf16[8,256,128]{2,1,0:T(8,128)(2,1)S(1)} %collective-permute-done.2.refs_0_) | copy-start | bytes 1572868
  57.1 13.6 %collective-permute-start.3 = (bf16[8,256,128]{2,1,0:T(8,128)(2,1)S(1)}, bf16[8,256,128]{2,1,0:T(8,128)(2,1)}, u32[]{:S(2)}, u32[]{:S(2)}) collective-permute-start(bf16[8,256,128]{2,1,0:T(8,128)(2,1)S(1)} %collective-permute-done.2.refs_0_), channel_id=1, source_target_pairs={{4,8},{5,1},{8,12},{9,5},{12,14},{13,9},{14,10},{15,13},{10,6},{11... | collective-permute-start | bytes 1572872 | tf_op jit(solution)/shard_map/ppermute | solution.py:341
  65.1 22.5 %collective-permute-start.12 = (bf16[8,256,128]{2,1,0:T(8,128)(2,1)S(1)}, bf16[8,256,128]{2,1,0:T(8,128)(2,1)}, u32[]{:S(2)}, u32[]{:S(2)}) collective-permute-start(bf16[8,256,128]{2,1,0:T(8,128)(2,1)S(1)} %collective-permute-done.1.refs_0_), channel_id=1, source_target_pairs={{0,1},{1,0},{2,3},{3,2},{4,5},{5,4},{6,7},{7,6},{8,9},{9,8},{10,11... | collective-permute-start | bytes 1572872 | tf_op jit(solution)/shard_map/ppermute | solution.py:342
  66.4 21.2 %collective-permute-start.11 = (bf16[8,256,128]{2,1,0:T(8,128)(2,1)S(1)}, bf16[8,256,128]{2,1,0:T(8,128)(2,1)}, u32[]{:S(2)}, u32[]{:S(2)}) collective-permute-start(bf16[8,256,128]{2,1,0:T(8,128)(2,1)S(1)} %collective-permute-done.7.refs_1_), channel_id=1, source_target_pairs={{0,1},{1,0},{2,3},{3,2},{4,5},{5,4},{6,7},{7,6},{8,9},{9,8},{10,11... | collective-permute-start | bytes 1572872 | tf_op jit(solution)/shard_map/ppermute | solution.py:342
  68.4 27.5 %collective-permute-start.10 = (bf16[8,256,128]{2,1,0:T(8,128)(2,1)S(1)}, bf16[8,256,128]{2,1,0:T(8,128)(2,1)}, u32[]{:S(2)}, u32[]{:S(2)}) collective-permute-start(bf16[8,256,128]{2,1,0:T(8,128)(2,1)S(1)} %collective-permute-done.2.refs_0_), channel_id=1, source_target_pairs={{0,1},{1,0},{2,3},{3,2},{4,5},{5,4},{6,7},{7,6},{8,9},{9,8},{10,11... | collective-permute-start | bytes 1572872 | tf_op jit(solution)/shard_map/ppermute | solution.py:342
  68.8 27.1 %collective-permute-start.9 = (bf16[8,256,128]{2,1,0:T(8,128)(2,1)}, bf16[8,256,128]{2,1,0:T(8,128)(2,1)}, u32[]{:S(2)}, u32[]{:S(2)}) collective-permute-start(bf16[8,256,128]{2,1,0:T(8,128)(2,1)} %collective-permute-done.8.refs_1_), channel_id=1, source_target_pairs={{0,1},{1,0},{2,3},{3,2},{4,5},{5,4},{6,7},{7,6},{8,9},{9,8},{10,11... | collective-permute-start | bytes 1572872 | tf_op jit(solution)/shard_map/ppermute | solution.py:342
  70.7 33.6 %collective-permute-start.4 = (bf16[8,256,128]{2,1,0:T(8,128)(2,1)}, bf16[8,256,128]{2,1,0:T(8,128)(2,1)}, u32[]{:S(2)}, u32[]{:S(2)}) collective-permute-start(bf16[8,256,128]{2,1,0:T(8,128)(2,1)} %collective-permute-done.3.refs_0_), channel_id=1, source_target_pairs={{0,1},{1,0},{2,3},{3,2},{4,5},{5,4},{6,7},{7,6},{8,9},{9,8},{10,11... | collective-permute-start | bytes 1572872 | tf_op jit(solution)/shard_map/ppermute | solution.py:342
  111.6 43.9 %collective-permute-start.16 = (f32[2,8,128]{2,1,0:T(8,128)S(1)}, f32[2,8,128]{2,1,0:T(8,128)S(1)}, u32[]{:S(2)}, u32[]{:S(2)}) collective-permute-start(f32[2,8,128]{2,1,0:T(8,128)S(1)} %get-tuple-element.9), channel_id=1, source_target_pairs={{1,0},{2,1},{3,2},{4,3},{5,4},{6,5},{7,6},{8,7},{9,8},{10,9},{11,1... | collective-permute-start | bytes 24584 | tf_op jit(solution)/shard_map/ppermute | solution.py:288
  113.6 41.9 %collective-permute-start.15 = (f32[2,8,128]{2,1,0:T(8,128)S(1)}, f32[2,8,128]{2,1,0:T(8,128)S(1)}, u32[]{:S(2)}, u32[]{:S(2)}) collective-permute-start(f32[2,8,128]{2,1,0:T(8,128)S(1)} %get-tuple-element.10), channel_id=1, source_target_pairs={{0,1},{1,2},{2,3},{3,4},{4,5},{5,6},{6,7},{7,8},{8,9},{9,10},{10,1... | collective-permute-start | bytes 24584 | tf_op jit(solution)/shard_map/ppermute | solution.py:287
  117.1 43.2 %copy-start.1 = (f32[16,31]{1,0:T(8,128)S(1)}, f32[16,31]{1,0:T(8,128)}, u32[]{:S(2)}) copy-start(f32[16,31]{1,0:T(8,128)} %param.11) | copy-start | bytes 5956
  155.5 0.6 copy-start.9
  156.1 0.6 copy-start.10
